TPU v7x, 32 devices: a whole 2x2x4 slice. The times are simulated.
32 devices in a mesh: pq: 2 (over x), rs: 16 (over z, y, core).
Axes of the slice: x: 2, y: 2, z: 4, core: 2. Of those that a mesh axis runs over, the one named last changes fastest.
Arguments:
- integrals: bfloat16 [128, 1152, 1152], P('pq', 'rs'), may hold values from -6 to 6
- coeff: bfloat16 [1152, 896], P('rs', 'pq'), may hold values from -0.1875 to 0.1875
Outputs:
- half_mo: bfloat16 [128, 896, 896], P('pq', 'rs')
All inputs are finite; a program needn't handle non-finite values.
Results may differ from a plain program's by a relative error of at most 0.0049.
Values may be sent and summed in bfloat16 or wider, within the bound.
A program may use at most 128 MiB of HBM per device.

v0:
```python
import functools
import math

import jax
import jax.numpy as jnp
from jax import lax
from jax.experimental import pallas as pl
from jax.experimental.pallas import tpu as pltpu
from jax.sharding import PartitionSpec as P

MESH = pl.DeviceIdType.MESH


def second_half(received, panel):
    return jnp.einsum("prl,rk->plk", received, panel, preferred_element_type=jnp.float32).astype(
        jnp.bfloat16
    )


def plain(integrals, panel):
    pair_rows, block_rows, nbasis = integrals.shape
    flat = integrals.reshape(pair_rows * block_rows, nbasis)
    first = jnp.dot(flat, panel, preferred_element_type=jnp.float32).astype(jnp.bfloat16)
    first = first.reshape(pair_rows, block_rows, panel.shape[1])
    return second_half(lax.all_to_all(first, "rs", split_axis=2, concat_axis=1, tiled=True), panel)


def fused_kernel(n, group, x_ref, c_ref, o_ref, tiles, parts, panel, send, recv, load_sem, send_sem, recv_sem, own_sem, hop_sem, part_sem):
    me = lax.axis_index("rs")
    col = lax.axis_index("pq")
    groups = send.shape[0]
    rows = send.shape[2]
    width = send.shape[3] // group
    nbasis = tiles.shape[3]
    half = n // 2
    far_side = lax.rem(me // half + 1, 2)
    near_side = me // half
    far = far_side * half
    near = near_side * half
    lines = n // 4
    core = lax.rem(me, 2)
    y = lax.rem(me // 2, 2)
    z = me // 4
    col_too = 1 - col
    columns = c_ref.shape[1]
    lead = 128
    leaders = lead // width

    def spot(at_z, at_y, at_core):
        return at_z * 4 + at_y * 2 + at_core

    def load(g):
        return pltpu.make_async_copy(x_ref.at[pl.ds(g * group, group)], tiles.at[g % 2], load_sem.at[g % 2])


    def far_partner(i):
        pair = lax.rem(lax.div(lax.rem(me, half), 2) + (i // 2 if isinstance(i, int) else lax.div(i, 2)), half // 2)
        return far + pair * 2 + lax.rem(me + i, 2)

    def partner(i):
        if not isinstance(i, int) or i < half:
            return far_partner(i)
        return near + lax.rem(me + i - half + 1, half)

    cuts = 3 if rows % 24 == 0 else 1
    short = rows // cuts

    def remote(g, i, at=0, count=rows):
        to = partner(i)
        return pltpu.make_async_remote_copy(
            src_ref=send.at[g, to, pl.ds(at, count)],
            dst_ref=recv.at[g, me, pl.ds(at, count)],
            send_sem=send_sem.at[g, i],
            recv_sem=recv_sem.at[g, i],
            device_id={"rs": to},
            device_id_type=MESH,
        )

    def own(g):
        return pltpu.make_async_copy(send.at[g, me], recv.at[g, me], own_sem.at[g])

    load(0).start()
    load(1).start()
    parts[col, me] = c_ref[...]
    barrier = pltpu.get_barrier_semaphore()
    for i in range(1, n):
        pl.semaphore_signal(barrier, inc=1, device_id={"rs": lax.rem(me + i, n)}, device_id_type=MESH)
    across_y = {"rs": spot(z, 1 - y, core)}
    across_x = {"pq": col_too}
    diagonal = {"pq": col_too, "rs": spot(z, 1 - y, core)}
    across_core = {"rs": spot(z, y, 1 - core)}
    for to in (across_x, diagonal):
        pl.semaphore_signal(barrier, inc=1, device_id=to, device_id_type=MESH)
    pl.semaphore_wait(barrier, n + 1)

    hops = []
    lanes = (pl.ds(0, lead), pl.ds(lead, columns - lead))

    def hop(s, q, r, to, sem):
        return pltpu.make_async_remote_copy(
            src_ref=parts.at[q, r, :, lanes[s]],
            dst_ref=parts.at[q, r, :, lanes[s]],
            send_sem=hop_sem.at[sem],
            recv_sem=part_sem.at[s, q, r],
            device_id=to,
            device_id_type=MESH,
        )

    def pass_on(s, q, r, *targets):
        for to in targets:
            copy = hop(s, q, r, to, len(hops))
            copy.start()
            hops.append(copy)

    def arrived(s, q, r):
        hop(s, q, r, across_x, 0).wait_recv()

    def along(k):
        return lax.rem(z + lines - k, lines)

    def arrived_from_core(s, q):
        for k in range(lines):
            for at_y in (0, 1):
                arrived(s, q, spot(k, at_y, 1 - core))

    for k in range(1, lines):
        pass_on(0, col, me, {"rs": spot(lax.rem(z + k, lines), y, core)})
    for k in range(lines):
        r = spot(along(k), y, core)
        if k:
            arrived(0, col, r)
        pass_on(0, col, r, across_y, across_x, diagonal, across_core)
    deep = lines // 2
    z_base = lax.div(z, deep) * deep
    opposite = lax.rem(z + deep, lines)
    o_base = lax.div(opposite, deep) * deep
    mates = [z_base + lax.rem(z + k, deep) for k in range(1, deep)]
    others = [o_base + lax.rem(z + k, deep) for k in range(1, deep)]
    pass_on(1, col, me, {"rs": spot(opposite, y, core)}, *({"rs": spot(m, y, core)} for m in mates))
    pass_on(1, col, me, across_y, across_x, across_core)
    for k in range(lines):
        mine, other = spot(along(k), y, core), spot(along(k), 1 - y, core)
        for q, r in ((col, other), (col_too, mine), (col_too, other)):
            arrived(0, q, r)
            pass_on(0, q, r, across_core)

    def weights(side, at, count):
        q = near_side if side else far_side
        return parts[q, :, :, at : at + count].reshape(nbasis, count)

    def ahead(g, cuts):
        load(g).wait()
        first_i = 2 * lax.rem(half // 2 - lax.div(lax.rem(me, half), 2), half // 2)
        count = rows // cuts
        for cut in range(cuts):
            block = tiles[g % 2, :, cut * count : (cut + 1) * count].reshape(group * count, nbasis)
            first = jnp.dot(block, weights(0, 0, lead), preferred_element_type=jnp.float32)
            for slot in range(group):
                piece = first[slot * count : (slot + 1) * count].astype(jnp.bfloat16)
                for d in range(-(-lead // width)):
                    end = min((d + 1) * width, lead)
                    send[g, far + d, cut * count : (cut + 1) * count, slot * width : slot * width + end - d * width] = piece[:, d * width : end]
            for j in range(leaders):
                remote(g, first_i + j, cut * count, count).start()

    def behind(g):
        first_i = 2 * lax.rem(half // 2 - lax.div(lax.rem(me, half), 2), half // 2)
        for q in range(group // step):
            block = tiles[g % 2, q * step : (q + 1) * step].reshape(step * rows, nbasis)
            first = jnp.dot(block, weights(0, lead, columns - lead), preferred_element_type=jnp.float32)
            for j in range(step):
                slot = q * step + j
                piece = first[j * rows : (j + 1) * rows].astype(jnp.bfloat16)
                for d in range(leaders, half):
                    start = max(d * width, lead)
                    send[g, far + d, :, slot * width + start - d * width : (slot + 1) * width] = piece[:, start - lead : (d + 1) * width - lead]
        for j in range(leaders, half):
            remote(g, lax.rem(first_i + j, half)).start()

    step = 4
    early = 2
    arrived_from_core(0, far_side)
    ahead(0, cuts)
    line = [z, *mates, opposite, *others]
    for k in range(1, lines):
        r = spot(line[k], y, core)
        arrived(1, col, r)
        if k == deep:
            pass_on(1, col, r, *({"rs": spot(m, y, core)} for m in mates))
        pass_on(1, col, r, across_y, across_x, across_core)
    ahead(1, 1)
    for k in range(lines):
        mine, other = spot(line[k], y, core), spot(line[k], 1 - y, core)
        arrived(1, col_too, mine)
        arrived(1, col, other)
        if k % 2:
            pass_on(1, col, other, across_x)
        else:
            pass_on(1, col_too, mine, across_y)
        pass_on(1, col_too, mine, across_core)
        pass_on(1, col, other, across_core)
    for k in range(lines):
        other = spot(line[k], 1 - y, core)
        arrived(1, col_too, other)
        pass_on(1, col_too, other, across_core)
    arrived_from_core(1, far_side)

    for g in range(groups):
        if 0 < g < groups - 1:
            load(g + 1).start()
        if g >= early:
            load(g).wait()
        for side in (0, 1):
            if side == 0 and g < early:
                behind(g)
                continue
            if g == 0:
                arrived_from_core(0, near_side)
                arrived_from_core(1, near_side)
            base = near if side else far
            for q in range(group // step):
                block = tiles[g % 2, q * step : (q + 1) * step].reshape(step * rows, nbasis)
                first = jnp.dot(block, weights(side, 0, columns), preferred_element_type=jnp.float32)
                for j in range(step):
                    slot = q * step + j
                    piece = first[j * rows : (j + 1) * rows].astype(jnp.bfloat16)
                    for d in range(half):
                        send[g, base + d, :, slot * width : (slot + 1) * width] = piece[:, d * width : (d + 1) * width]
            for i in range(half, n - 1) if side else range(half):
                remote(g, i).start()
        own(g).start()

    for q in (0, 1):
        panel[:, q * half * width : (q + 1) * half * width] = parts[q].reshape(nbasis, half * width)
    for copy in hops:
        copy.wait_send()

    contract = (((0,), (0,)), ((), ()))
    for g in range(groups):
        own(g).wait()
        if g + 1 < groups:
            for i in range(n - 1):
                remote(g, i).wait()
            lhs = recv[g].reshape(n * rows, group * width)
            out = lax.dot_general(lhs, panel[...], contract, preferred_element_type=jnp.float32)
        else:
            for i in range(half, n - 1):
                remote(g, i).wait()
            chunks = [(near, half)]
            for a in range(half // 2):
                pair = lax.rem(lax.rem(me, half) // 2 + half // 2 - a, half // 2)
                chunks.append((far + 2 * pair, 2))
            out = 0.0
            for at, (base, count) in enumerate(chunks):
                if at:
                    remote(g, 2 * at - 2).wait()
                    remote(g, 2 * at - 1).wait()
                lhs = recv[g, pl.ds(base, count)].reshape(count * rows, group * width)
                part = panel[pl.ds(pl.multiple_of(base * rows, 16), count * rows)]
                out += lax.dot_general(lhs, part, contract, preferred_element_type=jnp.float32)
        for j in range(group):
            o_ref[g * group + j] = out[j * width : (j + 1) * width].astype(jnp.bfloat16)


def fused(n, group, integrals, coeff):
    pair_rows, rows, nbasis = integrals.shape
    columns = coeff.shape[1]
    norb = 2 * columns
    width = norb // n
    groups = pair_rows // group
    flops = 2 * pair_rows * rows * nbasis * norb + 2 * pair_rows * width * n * rows * norb
    sent = 2 * pair_rows * rows * norb
    return pl.pallas_call(
        functools.partial(fused_kernel, n, group),
        out_shape=pltpu.VMEM((pair_rows, width, norb), jnp.bfloat16),
        in_specs=[pl.BlockSpec(memory_space=pl.ANY), pl.BlockSpec(memory_space=pltpu.VMEM)],
        out_specs=pl.BlockSpec(memory_space=pltpu.VMEM),
        scratch_shapes=[
            pltpu.VMEM((2, group, rows, nbasis), jnp.bfloat16),
            pltpu.VMEM((2, n, rows, columns), jnp.bfloat16),
            pltpu.VMEM((nbasis, norb), jnp.bfloat16),
            pltpu.VMEM((groups, n, rows, group * width), jnp.bfloat16),
            pltpu.VMEM((groups, n, rows, group * width), jnp.bfloat16),
            pltpu.SemaphoreType.DMA((2,)),
            pltpu.SemaphoreType.DMA((groups, n)),
            pltpu.SemaphoreType.DMA((groups, n)),
            pltpu.SemaphoreType.DMA((groups,)),
            pltpu.SemaphoreType.DMA((5 * n,)),
            pltpu.SemaphoreType.DMA((2, 2, n)),
        ],
        compiler_params=pltpu.CompilerParams(
            collective_id=0, has_side_effects=True, vmem_limit_bytes=50 * 2**20
        ),
        cost_estimate=pl.CostEstimate(flops=flops, bytes_accessed=4 * sent, transcendentals=0),
    )(integrals, coeff)


def on_device(n, splits, integrals, coeff):
    pair_rows, rows, nbasis = integrals.shape
    columns = coeff.shape[1]
    norb = columns * splits
    width = norb // n
    group = math.lcm(4, 128 // math.gcd(width, 128))
    aligned = rows % 8 == 0 and width % 8 == 0 and pair_rows % group == 0 and pair_rows >= 2 * group
    if splits == 2 and n % 8 == 0 and aligned and group * width <= 2048 and 2 * width <= 128 < columns:
        return fused(n, group, integrals, coeff)
    strip = lax.all_gather(coeff, "pq", axis=1, tiled=True)
    return plain(integrals, lax.all_gather(strip, "rs", axis=0, tiled=True))


def solution(mesh):
    placed = (P("pq", "rs", None), P("rs", "pq"))
    return jax.shard_map(
        functools.partial(on_device, mesh.shape["rs"], mesh.shape["pq"]),
        mesh=mesh,
        in_specs=placed,
        out_specs=P("pq", "rs", None),
        check_vma=False,
    )
```

profile of v0, /device:TPU:13, one launch (start us, length us, event | category | flops | bytes accessed | tf_op | source)
XLA Modules:
  0.0 204.2 jit_solution(18357675269345739303)
XLA Ops:
  0.0 201.4 %shard_map.28 = bf16[64,56,896]{2,1,0:T(8,128)(2,1)S(1)} custom-call(bf16[64,72,1152]{2,1,0:T(8,128)(2,1)} %x_ref.1, bf16[72,448]{1,0:T(8,128)(2,1)} %c_ref.1), custom_call_target="tpu_custom_call" | custom-call | flops 16911433728 | bytes 33030144 | tf_op jit(solution)/shard_map/pallas_call | solution.py:273
  201.4 2.7 %copy.4 = bf16[64,56,896]{2,1,0:T(8,128)(2,1)} copy(bf16[64,56,896]{2,1,0:T(8,128)(2,1)S(1)} %shard_map.28) | data formatting | bytes 12845056
where the time goes:
time: 204 us
  Pallas kernels  201 us (99%)
  local copies, waits for them, and re-layouts  2.75 us (1%)
    pallas_call x1, Pallas kernels, fused(): pl.pallas_call(functools.partial(fused_kernel, n, group), out_shape=pltpu...  201 us

commit v1 on v0

--- a/solution.py
+++ b/solution.py
@@ -25,7 +25,7 @@
     return second_half(lax.all_to_all(first, "rs", split_axis=2, concat_axis=1, tiled=True), panel)
 
 
-def fused_kernel(n, group, x_ref, c_ref, o_ref, tiles, parts, panel, send, recv, load_sem, send_sem, recv_sem, own_sem, hop_sem, part_sem):
+def fused_kernel(n, group, x_ref, c_ref, o_ref, tiles, parts, panel, send, recv, load_sem, send_sem, recv_sem, own_sem, hop_sem, part_sem, local_sem):
     me = lax.axis_index("rs")
     col = lax.axis_index("pq")
     groups = send.shape[0]
@@ -62,9 +62,6 @@
             return far_partner(i)
         return near + lax.rem(me + i - half + 1, half)
 
-    cuts = 3 if rows % 24 == 0 else 1
-    short = rows // cuts
-
     def remote(g, i, at=0, count=rows):
         to = partner(i)
         return pltpu.make_async_remote_copy(
@@ -79,9 +76,8 @@
     def own(g):
         return pltpu.make_async_copy(send.at[g, me], recv.at[g, me], own_sem.at[g])
 
-    load(0).start()
-    load(1).start()
-    parts[col, me] = c_ref[...]
+    local = pltpu.make_async_copy(c_ref, parts.at[col, me], local_sem)
+    local.start()
     barrier = pltpu.get_barrier_semaphore()
     for i in range(1, n):
         pl.semaphore_signal(barrier, inc=1, device_id={"rs": lax.rem(me + i, n)}, device_id_type=MESH)
@@ -91,6 +87,9 @@
     across_core = {"rs": spot(z, y, 1 - core)}
     for to in (across_x, diagonal):
         pl.semaphore_signal(barrier, inc=1, device_id=to, device_id_type=MESH)
+    load(0).start()
+    load(1).start()
+    local.wait()
     pl.semaphore_wait(barrier, n + 1)
 
     hops = []
@@ -151,17 +150,16 @@
     def ahead(g, cuts):
         load(g).wait()
         first_i = 2 * lax.rem(half // 2 - lax.div(lax.rem(me, half), 2), half // 2)
-        count = rows // cuts
-        for cut in range(cuts):
-            block = tiles[g % 2, :, cut * count : (cut + 1) * count].reshape(group * count, nbasis)
+        for at, count in cuts:
+            block = tiles[g % 2, :, at : at + count].reshape(group * count, nbasis)
             first = jnp.dot(block, weights(0, 0, lead), preferred_element_type=jnp.float32)
             for slot in range(group):
                 piece = first[slot * count : (slot + 1) * count].astype(jnp.bfloat16)
                 for d in range(-(-lead // width)):
                     end = min((d + 1) * width, lead)
-                    send[g, far + d, cut * count : (cut + 1) * count, slot * width : slot * width + end - d * width] = piece[:, d * width : end]
+                    send[g, far + d, at : at + count, slot * width : slot * width + end - d * width] = piece[:, d * width : end]
             for j in range(leaders):
-                remote(g, first_i + j, cut * count, count).start()
+                remote(g, first_i + j, at, count).start()
 
     def behind(g):
         first_i = 2 * lax.rem(half // 2 - lax.div(lax.rem(me, half), 2), half // 2)
@@ -174,13 +172,13 @@
                 for d in range(leaders, half):
                     start = max(d * width, lead)
                     send[g, far + d, :, slot * width + start - d * width : (slot + 1) * width] = piece[:, start - lead : (d + 1) * width - lead]
-        for j in range(leaders, half):
-            remote(g, lax.rem(first_i + j, half)).start()
+        for idx in range(half - leaders):
+            remote(g, idx + leaders * (idx >= first_i).astype(jnp.int32)).start()
 
     step = 4
     early = 2
     arrived_from_core(0, far_side)
-    ahead(0, cuts)
+    ahead(0, ((0, 8), (8, 24), (32, rows - 32)) if rows > 32 else ((0, rows),))
     line = [z, *mates, opposite, *others]
     for k in range(1, lines):
         r = spot(line[k], y, core)
@@ -188,7 +186,7 @@
         if k == deep:
             pass_on(1, col, r, *({"rs": spot(m, y, core)} for m in mates))
         pass_on(1, col, r, across_y, across_x, across_core)
-    ahead(1, 1)
+    ahead(1, ((0, rows),))
     for k in range(lines):
         mine, other = spot(line[k], y, core), spot(line[k], 1 - y, core)
         arrived(1, col_too, mine)
@@ -210,7 +208,7 @@
             load(g + 1).start()
         if g >= early:
             load(g).wait()
-        for side in (0, 1):
+        for side in (0, 1) if g + 1 < groups else (1, 0):
             if side == 0 and g < early:
                 behind(g)
                 continue
@@ -273,7 +271,7 @@
     return pl.pallas_call(
         functools.partial(fused_kernel, n, group),
         out_shape=pltpu.VMEM((pair_rows, width, norb), jnp.bfloat16),
-        in_specs=[pl.BlockSpec(memory_space=pl.ANY), pl.BlockSpec(memory_space=pltpu.VMEM)],
+        in_specs=[pl.BlockSpec(memory_space=pl.ANY), pl.BlockSpec(memory_space=pl.ANY)],
         out_specs=pl.BlockSpec(memory_space=pltpu.VMEM),
         scratch_shapes=[
             pltpu.VMEM((2, group, rows, nbasis), jnp.bfloat16),
@@ -287,6 +285,7 @@
             pltpu.SemaphoreType.DMA((groups,)),
             pltpu.SemaphoreType.DMA((5 * n,)),
             pltpu.SemaphoreType.DMA((2, 2, n)),
+            pltpu.SemaphoreType.DMA,
         ],
         compiler_params=pltpu.CompilerParams(
             collective_id=0, has_side_effects=True, vmem_limit_bytes=50 * 2**20

time: 204 us -> 201 us (0.985); the launches traced: 204 us -> 198 us
  Pallas kernels: 201 us -> 195 us
    pallas_call x1, Pallas kernels: 201 us -> 195 us  [fused(): pl.pallas_call(functools.partial(fused_kernel, n, group), out_shape=pltpu...]
where the time goes in v1:
time: 201 us; the launch traced here: 198 us
  Pallas kernels  195 us (97%)
  local copies, waits for them, and re-layouts  2.75 us (1%)
    pallas_call x1, Pallas kernels, fused(): pl.pallas_call(functools.partial(fused_kernel, n, group), out_shape=pltpu...  195 us

profile of v1, /device:TPU:13, one launch (start us, length us, event | category | flops | bytes accessed | tf_op | source)
XLA Modules:
  0.0 197.6 jit_solution(13852344888523937639)
XLA Ops:
  0.0 194.8 %shard_map.28 = bf16[64,56,896]{2,1,0:T(8,128)(2,1)S(1)} custom-call(bf16[64,72,1152]{2,1,0:T(8,128)(2,1)} %x_ref.1, bf16[72,448]{1,0:T(8,128)(2,1)} %c_ref.1), custom_call_target="tpu_custom_call" | custom-call | flops 16911433728 | bytes 33030144 | tf_op jit(solution)/shard_map/pallas_call | solution.py:271
  194.8 2.7 %copy.4 = bf16[64,56,896]{2,1,0:T(8,128)(2,1)} copy(bf16[64,56,896]{2,1,0:T(8,128)(2,1)S(1)} %shard_map.28) | data formatting | bytes 12845056
